TPU v7x, 16 devices: a whole 2x2x2 slice. The times are simulated.
16 devices in a mesh: dp: 16 (over z, y, x, core).
Axes of the slice: x: 2, y: 2, z: 2, core: 2. Of those that a mesh axis runs over, the one named last changes fastest.
Arguments:
- grad_rows: bfloat16 [16, 14147584], P('dp')
- master: float32 [14147584], P('dp')
- mom_first: float32 [14147584], P('dp')
- mom_second: float32 [14147584], P('dp')
- decay_mask: int32 [14147584], P('dp')
- learn_rate: float32 [1], replicated
Outputs:
- output 1: bfloat16 [14147584], replicated
- output 2: float32 [14147584], P('dp')
- output 3: float32 [14147584], P('dp')
- output 4: float32 [14147584], P('dp')
- output 5: float32 [1], replicated
All inputs are finite; a program needn't handle non-finite values.
Results may differ from a plain program's by a relative error of at most 0.001.
Values are sent between devices in bfloat16 or wider.
A program may use at most 1 GiB of HBM per device.

v0:
```python
import jax
import jax.numpy as jnp
from jax import lax
from jax.sharding import PartitionSpec as P, NamedSharding

BETA_FIRST = 0.9
BETA_SECOND = 0.95
ADAM_EPS = 1e-8
CLIP_EPS = 1e-6
WEIGHT_DECAY = 0.1
ADAM_STEP = 10


def adamw_block(grad_mean, grad_norm, master, mom_first, mom_second, decay_mask, learn_rate):
    clip_coef = jnp.minimum(1.0, 1.0 / (grad_norm + CLIP_EPS))
    clipped = grad_mean * clip_coef
    new_first = BETA_FIRST * mom_first + (1.0 - BETA_FIRST) * clipped
    new_second = BETA_SECOND * mom_second + (1.0 - BETA_SECOND) * clipped * clipped
    step_dir = (new_first / (1.0 - BETA_FIRST ** ADAM_STEP)) / (jnp.sqrt(new_second / (1.0 - BETA_SECOND ** ADAM_STEP)) + ADAM_EPS)
    decay_flag = decay_mask.astype(jnp.float32)
    new_master = master - learn_rate[0] * (step_dir + WEIGHT_DECAY * decay_flag * master)
    return new_master, new_first, new_second


def solution(mesh):
    num_dev = mesh.shape['dp']

    def local_step(grad_row, master, mom_first, mom_second, decay_mask, learn_rate):
        shard_len = master.shape[0]
        grad_parts = grad_row.reshape(num_dev, shard_len)
        received = lax.all_to_all(grad_parts, 'dp', 0, 0, tiled=True)
        grad_mean = jnp.sum(received, axis=0, dtype=jnp.float32) / num_dev
        sq_total = lax.psum(jnp.sum(grad_mean * grad_mean), 'dp')
        grad_norm = jnp.sqrt(sq_total)
        new_master, new_first, new_second = adamw_block(grad_mean, grad_norm, master, mom_first, mom_second, decay_mask, learn_rate)
        params = lax.all_gather(new_master.astype(jnp.bfloat16), 'dp', tiled=True)
        return params, new_master, new_first, new_second, grad_norm.reshape(1)

    return jax.shard_map(local_step, mesh=mesh, in_specs=(P('dp', None), P('dp'), P('dp'), P('dp'), P('dp'), P()), out_specs=(P(), P('dp'), P('dp'), P('dp'), P()), check_vma=False)
```

profile of v0, /device:TPU:0, one launch (start us, length us, event | category | flops | bytes accessed | tf_op | source)
XLA Modules:
  0.0 1302.7 jit_solution(13184134956915883487)
XLA Ops:
  7.2 0.0 all-gather.3.cloned.1.call-start
  7.2 0.5 broadcast.13
  7.7 166.4 %reduce.2 = bf16[16,884224]{1,0:T(8,128)(2,1)} reduce(bf16[16,1,884224]{2,1,0:T(2,128)(2,1)} %bitcast.4, bf16[]{:T(256)} %broadcast.13), dimensions={1}, to_apply=%bitcast.1.reduce_sub_computation | reduce | bytes 56590336 | tf_op jit(solution)/shard_map/all_to_all | solution.py:31
  174.1 97.7 %reshape.22 = bf16[16,2,442112]{2,1,0:T(2,128)(2,1)} reshape(bf16[16,884224]{1,0:T(8,128)(2,1)} %reduce.2) | data formatting | bytes 56590336
  271.8 314.9 %all_to_all.9 = bf16[16,2,442112]{2,1,0:T(2,128)(2,1)} all-to-all(bf16[16,2,442112]{2,1,0:T(2,128)(2,1)} %reshape.22), channel_id=1, replica_groups=mesh['dp'=16] {'dp'}, dimensions={0} | all-to-all | bytes 56590336 | tf_op jit(solution)/shard_map/all_to_all | solution.py:31
  586.7 54.1 %reshape.23 = bf16[16,1,884224]{2,1,0:T(2,128)(2,1)} reshape(bf16[16,2,442112]{2,1,0:T(2,128)(2,1)} %all_to_all.9) | data formatting | bytes 56590336
  640.8 148.2 %convert_reduce_fusion = f32[884224]{0:T(1024)S(1)} fusion(bf16[16,1,884224]{2,1,0:T(2,128)(2,1)} %reshape.23), kind=kLoop, calls=%fused_computation | loop fusion | flops 27410944 | bytes 31832064 | tf_op jit(solution)/shard_map/reduce_sum | solution.py:32
  789.0 1.5 multiply_reduce_fusion
  791.2 36.0 %psum.7 = f32[]{:T(128)} all-reduce(f32[]{:T(128)} %multiply_reduce_fusion), channel_id=1, replica_groups=mesh['dp'=16] {'dp'}, use_global_device_ids=true, to_apply=%region_2.0 | all-reduce | flops 1 | bytes 8 | tf_op jit(solution)/shard_map/psum | solution.py:33
  827.9 9.3 fusion.1
  837.2 20.9 %reshape.19 = bf16[1,1,884224]{2,1,0:T(2,128)(2,1)} reshape(bf16[884224]{0:T(1024)(128)(2,1)S(1)} %get-tuple-element.5) | data formatting | bytes 3536896
  858.1 0.0 all-gather.3.cloned.1.call-update
  858.1 208.0 %all-gather.3.cloned.1.call-done = bf16[16,1,884224]{2,1,0:T(2,128)(2,1)} async-done(((bf16[1,1,884224]{2,1,0:T(2,128)(2,1)}), bf16[16,1,884224]{2,1,0:T(2,128)(2,1)}) %all-gather.3.cloned.1.call-update) | async-done | bytes 28295184 | tf_op jit(solution)/shard_map/all_gather | solution.py:36
  1066.2 165.7 %reduce.1 = bf16[16,884224]{1,0:T(8,128)(2,1)} reduce(bf16[16,1,884224]{2,1,0:T(2,128)(2,1)} %all-gather.3.cloned.1.call-done, bf16[]{:T(256)} %constant.26), dimensions={1}, to_apply=%all-gather.reduce_sub_computation | reduce | bytes 56590336 | tf_op jit(solution)/shard_map/all_gather | solution.py:36
  1231.9 62.6 %reshape.20 = bf16[14147584]{0:T(1024)(128)(2,1)} reshape(bf16[16,884224]{1,0:T(8,128)(2,1)} %reduce.1) | data formatting | bytes 56590336
Async XLA Ops:
  7.2 1059.0 %all-gather.3.cloned.1.call-start = ((), (), s32[]{:S(2)}) async-start(), calls=%async_computation.1 | async-start | bytes 60127232 | tf_op jit(solution)/shard_map/all_gather | solution.py:36
Sparse Core Ops, SparseCore 0:
  858.3 207.8 all-gather.2
where the time goes:
time: 1310 us; the launch traced here: 1300 us
  other arithmetic  491 us (37%)
  blocking collectives  351 us (27%)
  local copies, waits for them, and re-layouts  236 us (18%)
  waiting for transfers between devices  208 us (16%)
  between operations  16.7 us (1%)
    all_to_all x1, blocking collectives, local_step(): received = lax.all_to_all(grad_parts, 'dp', 0, 0, tiled=True)  315 us
    unnamed x4, local copies, waits for them, and re-layouts  235 us
    all_gather x1, waiting for transfers between devices, local_step(): params = lax.all_gather(new_master.astype(jnp.bfloat16), 'dp', tiled=True)  208 us
    all_to_all x1, other arithmetic, local_step(): received = lax.all_to_all(grad_parts, 'dp', 0, 0, tiled=True)  166 us
    all_gather x1, other arithmetic, local_step(): params = lax.all_gather(new_master.astype(jnp.bfloat16), 'dp', tiled=True)  166 us
    reduce_sum x1, other arithmetic, local_step(): grad_mean = jnp.sum(received, axis=0, dtype=jnp.float32) / num_dev  148 us
    psum x1, blocking collectives, local_step(): sq_total = lax.psum(jnp.sum(grad_mean * grad_mean), 'dp')  36 us
  transfers between devices with their start and end apart: 1, of which 1 were waited for; matrix products, arithmetic and copies ran while one was open for 0% of the time, Pallas kernels for 0%

commit v1 on v0

v1 whole, which is shorter than its diff:
```python
import jax
import jax.numpy as jnp
from jax import lax
from jax.experimental import pallas as pl
from jax.experimental.pallas import tpu as pltpu
from jax.sharding import PartitionSpec as P

BETA_FIRST = 0.9
BETA_SECOND = 0.95
ADAM_EPS = 1e-8
CLIP_EPS = 1e-6
WEIGHT_DECAY = 0.1
ADAM_STEP = 10

NDEV = 16
LANES = 128
ROWS = 6908
ROWS_PAD = 6912
CHUNKS = 12
CR = 576
CW = CR * LANES
SLAB = 72
NSLAB = CR // SLAB
DEPTH = 4
UNITS = ROWS // 4
PART_UNIT0 = (0, 576, 1152)
PART_COUNT = (4, 4, 5)
PART_UNITS = (144, 144, 115)
PART_BASE = (0, 4, 8)
AG_CHUNKS = 13

MESH = pl.DeviceIdType.MESH


def weight(axis):
    return 2 + axis + axis * axis


def step_of(me, axis):
    w = weight(axis)
    return (1 - 2 * ((me // w) % 2)) * w


def chunk_row(q):
    return CR * q - 4 * (q // (CHUNKS - 1))


def remote(src, dst, ssem, rsem, dev):
    return pltpu.make_async_remote_copy(src_ref=src, dst_ref=dst, send_sem=ssem, recv_sem=rsem, device_id=(dev,), device_id_type=MESH)


def rs_kernel(grad, gout, parts_out, prow, own, par, sb, r1, r2, r3, acc, nrm, psend, precv, s1s, s1r, s2s, s2r, s3s, s3r, ns, nr, lo, lp):
    me = lax.axis_index('dp')
    core = me % 2
    partner = me + 1 - 2 * core

    barrier = pltpu.get_barrier_semaphore()

    def greet(i, _):
        other = lax.rem(me + i, NDEV)
        pl.semaphore_signal(barrier, inc=1, device_id=(other,), device_id_type=MESH)
        return 0

    lax.fori_loop(1, NDEV, greet, 0)
    pl.semaphore_wait(barrier, NDEV - 1)

    def decode(phase, t):
        p = t % 3
        j = t // 3
        if phase == 1:
            o1, o2, o3, k = 1, j % 2, (j // 2) % 2, j // 4
        elif phase == 2:
            o1, o2, o3, k = 0, 1, j % 2, j // 2
        elif phase == 3:
            o1, o2, o3, k = 0, 0, 1, j
        else:
            o1, o2, o3, k = 0, 0, 0, j
        a1, a2, a3 = p, (p + 1) % 3, (p + 2) % 3
        shift = o1 * step_of(me, a1) + o2 * step_of(me, a2) + o3 * step_of(me, a3)
        return p, j, k, a1, a2, a3, shift, 4 * p + k

    base_of = {1: 0, 2: 48, 3: 72, 4: 84}
    count_of = {1: 48, 2: 24, 3: 12, 4: 12}

    def grad_slice(block, q):
        start = pl.multiple_of((block * ROWS + chunk_row(q)) * LANES, LANES)
        return grad.at[:, pl.ds(start, CW)]

    def partner_copy(phase, t):
        _, _, _, _, _, _, shift, q = decode(phase, t)
        s = base_of[phase] + t
        return remote(grad_slice(partner + shift, q), prow.at[s], psend.at[s], precv.at[s], partner)

    for phase in (1, 2, 3, 4):
        def send_rows(t, _, phase=phase):
            partner_copy(phase, t).start()
            return 0
        lax.fori_loop(0, count_of[phase], send_rows, 0)

    def loads(phase, t):
        _, _, _, _, _, _, shift, q = decode(phase, t)
        slot = t % DEPTH
        return (pltpu.make_async_copy(grad_slice(me + shift, q), own.at[slot], lo.at[slot]),
                pltpu.make_async_copy(prow.at[base_of[phase] + t], par.at[slot], lp.at[slot]))

    def start_loads(phase, t):
        partner_copy(phase, t).wait_recv()
        a, b = loads(phase, t)
        a.start()
        b.start()

    def chip_sum(slot, i):
        lo_col = i * SLAB * LANES
        if not isinstance(lo_col, int):
            lo_col = pl.multiple_of(lo_col, SLAB * LANES)
        cols = pl.ds(lo_col, SLAB * LANES)
        v = own[slot, :, cols].astype(jnp.float32) + par[slot, :, cols].astype(jnp.float32)
        return v.reshape(SLAB, LANES)

    def s1_copy(t):
        p, j, k, a1, a2, a3, _, q = decode(1, t)
        return remote(sb.at[t], r1.at[t], s1s.at[t], s1r.at[t], me + step_of(me, a1))

    def r1_at(p, k, o2, o3):
        return ((k * 4) + o3 * 2 + o2) * 3 + p

    def r2_at(p, k, o3):
        return (k * 2 + o3) * 3 + p

    def s2_copy(t):
        p, j, k, a1, a2, a3, _, q = decode(2, t)
        return remote(r1.at[r1_at(p, k, 1, j % 2)], r2.at[t], s2s.at[t], s2r.at[t], me + step_of(me, a2))

    def s3_copy(t):
        p, j, k, a1, a2, a3, _, q = decode(3, t)
        return remote(r2.at[r2_at(p, k, 1)], r3.at[t], s3s.at[t], s3r.at[t], me + step_of(me, a3))

    def run_phase(phase, body, last=None):
        n = count_of[phase]
        for t in range(DEPTH - 1):
            start_loads(phase, t)

        def one(t, _):
            @pl.when(t + DEPTH - 1 < n)
            def _():
                start_loads(phase, t + DEPTH - 1)
            a, b = loads(phase, t)
            a.wait()
            b.wait()
            body(t)
            return 0

        lax.fori_loop(0, n if last is None else n - 1, one, 0)
        if last is not None:
            a, b = loads(phase, n - 1)
            a.wait()
            b.wait()
            last(n - 1)

    def slabs(fn):
        def one(i, _):
            fn(i, pl.ds(pl.multiple_of(i * SLAB, SLAB), SLAB))
            return 0
        lax.fori_loop(0, NSLAB, one, 0)

    def phase1(t):
        slot = t % DEPTH

        def fn(i, rows):
            sb[t, rows, :] = chip_sum(slot, i)
        slabs(fn)
        s1_copy(t).start()

    def phase2(t):
        slot = t % DEPTH
        p, j, k, *_ = decode(2, t)
        src = r1_at(p, k, 1, j % 2)
        s1_copy(src).wait_recv()

        def fn(i, rows):
            r1[src, rows, :] = chip_sum(slot, i) + r1[src, rows, :]
        slabs(fn)
        s2_copy(t).start()

    def phase3(t):
        slot = t % DEPTH
        p, j, k, *_ = decode(3, t)
        s1 = r1_at(p, k, 0, 1)
        s2 = r2_at(p, k, 1)
        s1_copy(s1).wait_recv()
        s2_copy(s2).wait_recv()

        def fn(i, rows):
            r2[s2, rows, :] = chip_sum(slot, i) + r1[s1, rows, :] + r2[s2, rows, :]
        slabs(fn)
        s3_copy(t).start()

    acc[...] = jnp.zeros_like(acc)

    def final_sum(t):
        slot = t % DEPTH
        p, j, k, *_ = decode(4, t)
        s1 = r1_at(p, k, 0, 0)
        s2 = r2_at(p, k, 0)
        s1_copy(s1).wait_recv()
        s2_copy(s2).wait_recv()
        s3_copy(t).wait_recv()

        def value(i, rows):
            v = chip_sum(slot, i) + r1[s1, rows, :] + r2[s2, rows, :] + r3[t, rows, :]
            return v * (1.0 / NDEV)
        return value, 4 * p + k

    def phase4(t):
        value, q = final_sum(t)

        def fn(i, rows):
            v = value(i, rows)
            gout[pl.ds(pl.multiple_of(q * CR + i * SLAB, 8), SLAB), :] = v
            acc[...] += jnp.sum((v * v).reshape(SLAB // 8, 8, LANES), axis=0)
        slabs(fn)

    def phase4_last(t):
        value, _ = final_sum(t)
        start = chunk_row(CHUNKS - 1)
        for i in range(NSLAB):
            v = value(i, pl.ds(i * SLAB, SLAB))
            gout[start + i * SLAB:start + (i + 1) * SLAB, :] = v
            sq = v * v
            if i == 0:
                row = lax.broadcasted_iota(jnp.int32, (SLAB, LANES), 0)
                sq = jnp.where(row < 4, 0.0, sq)
            acc[...] += jnp.sum(sq.reshape(SLAB // 8, 8, LANES), axis=0)

    run_phase(1, phase1)
    run_phase(2, phase2)
    run_phase(3, phase3)
    run_phase(4, phase4, phase4_last)

    nrm[me] = acc[...]

    def norm_copy(i):
        other = lax.rem(me + i, NDEV)
        return remote(acc, nrm.at[me], ns.at[i], nr.at[me], other)

    def norm_arrival(i):
        other = lax.rem(me + i, NDEV)
        return remote(acc, nrm.at[other], ns.at[i], nr.at[other], other)

    def norm_send(i, _):
        norm_copy(i).start()
        return 0

    def norm_wait(i, _):
        norm_arrival(i).wait_recv()
        return 0

    lax.fori_loop(1, NDEV, norm_send, 0)

    def drain(n, copy):
        def one(t, _):
            copy(t).wait_send()
            return 0
        lax.fori_loop(0, n, one, 0)

    for phase in (1, 2, 3, 4):
        drain(count_of[phase], lambda t, phase=phase: partner_copy(phase, t))
    drain(48, s1_copy)
    drain(24, s2_copy)
    drain(12, s3_copy)
    lax.fori_loop(1, NDEV, norm_wait, 0)
    drain(NDEV - 1, lambda t: norm_copy(t + 1))
    total = nrm[0]
    for d in range(1, NDEV):
        total = total + nrm[d]
    parts_out[...] = total


def reduce_scatter(grad):
    f32 = jnp.float32
    dma = pltpu.SemaphoreType.DMA
    return pl.pallas_call(
        rs_kernel,
        out_shape=(jax.ShapeDtypeStruct((ROWS_PAD, LANES), f32), jax.ShapeDtypeStruct((8, LANES), f32), jax.ShapeDtypeStruct((96, 1, CW), jnp.bfloat16)),
        in_specs=[pl.BlockSpec(memory_space=pl.ANY)],
        out_specs=(pl.BlockSpec(memory_space=pltpu.VMEM), pl.BlockSpec(memory_space=pltpu.VMEM), pl.BlockSpec(memory_space=pl.ANY)),
        scratch_shapes=[
            pltpu.VMEM((DEPTH, 1, CW), jnp.bfloat16),
            pltpu.VMEM((DEPTH, 1, CW), jnp.bfloat16),
            pltpu.VMEM((48, CR, LANES), f32),
            pltpu.VMEM((48, CR, LANES), f32),
            pltpu.VMEM((24, CR, LANES), f32),
            pltpu.VMEM((12, CR, LANES), f32),
            pltpu.VMEM((8, LANES), f32),
            pltpu.VMEM((NDEV, 8, LANES), f32),
            dma((96,)), dma((96,)),
            dma((48,)), dma((48,)),
            dma((24,)), dma((24,)),
            dma((12,)), dma((12,)),
            dma((NDEV,)), dma((NDEV,)),
            dma((DEPTH,)), dma((DEPTH,)),
        ],
        compiler_params=pltpu.CompilerParams(collective_id=0, has_side_effects=True, vmem_limit_bytes=56 * 1024 * 1024),
        name='reduce_scatter',
    )(grad)


def adam_kernel(lr, parts, g, w, m, v, mask, p_out, w_out, m_out, v_out, norm_out):
    norm = jnp.sqrt(jnp.sum(parts[...], keepdims=True))
    norm_out[...] = jnp.broadcast_to(norm, norm_out.shape)
    clip = jnp.minimum(1.0, 1.0 / (norm + CLIP_EPS))
    h = g[...] * clip
    m_new = BETA_FIRST * m[...] + (1.0 - BETA_FIRST) * h
    v_new = BETA_SECOND * v[...] + (1.0 - BETA_SECOND) * h * h
    step_dir = (m_new / (1.0 - BETA_FIRST ** ADAM_STEP)) / (jnp.sqrt(v_new / (1.0 - BETA_SECOND ** ADAM_STEP)) + ADAM_EPS)
    old = w[...]
    w_new = old - lr[0] * (step_dir + WEIGHT_DECAY * mask[...].astype(jnp.float32) * old)
    w_out[...] = w_new
    m_out[...] = m_new
    v_out[...] = v_new
    p_out[...] = w_new.astype(jnp.bfloat16)


def adam(lr, parts, g, w, m, v, mask):
    f32 = jnp.float32
    block = pl.BlockSpec((CR, LANES), lambda i: (i, 0))
    whole = pl.BlockSpec((8, LANES), lambda i: (0, 0))
    flat = lambda a: a.reshape(ROWS, LANES)
    state = jax.ShapeDtypeStruct((ROWS, LANES), f32)
    return pl.pallas_call(
        adam_kernel,
        grid=(CHUNKS,),
        out_shape=(jax.ShapeDtypeStruct((ROWS_PAD, LANES), jnp.bfloat16), state, state, state, jax.ShapeDtypeStruct((8, LANES), f32)),
        in_specs=[pl.BlockSpec(memory_space=pltpu.SMEM), whole, block, block, block, block, block],
        out_specs=(block, block, block, block, whole),
        name='adam',
    )(lr, parts, g, flat(w), flat(m), flat(v), flat(mask))


def ag_kernel(mine, out, is_, ir, ds_, dr, lsem):
    me = lax.axis_index('dp')
    partner = me + 1 - 2 * (me % 2)
    barrier = pltpu.get_barrier_semaphore()
    near = [me + step_of(me, a) for a in range(3)]
    for other in near + [partner]:
        pl.semaphore_signal(barrier, inc=1, device_id=(other,), device_id_type=MESH)
    pl.semaphore_wait(barrier, 4)

    def place(p, k, n, dev=me):
        a = [p, (p + 1) % 3, (p + 2) % 3]
        block = dev
        for bit in range(3):
            if (n >> bit) & 1:
                block = block + step_of(me, a[bit])
        return out.at[pl.ds(block * UNITS + PART_UNIT0[p] + PART_UNITS[p] * k, PART_UNITS[p])]

    def source(p, k, n):
        if n == 0:
            return mine.at[pl.ds(PART_UNIT0[p] + PART_UNITS[p] * k, PART_UNITS[p])]
        return place(p, k, n)

    def ici(p, k, hop, n):
        slot = n | (1 << hop)
        c = PART_BASE[p] + k
        return remote(source(p, k, n), place(p, k, n), is_.at[slot, c], ir.at[slot, c], near[(p + hop) % 3])

    def ici_arrival(p, k, n):
        hop = n.bit_length() - 1
        c = PART_BASE[p] + k
        return remote(place(p, k, n), place(p, k, n), is_.at[n, c], ir.at[n, c], near[(p + hop) % 3])

    def die(p, k, n):
        c = PART_BASE[p] + k
        return remote(source(p, k, n), place(p, k, n), ds_.at[n, c], dr.at[n, c], partner)

    def die_arrival(p, k, n):
        c = PART_BASE[p] + k
        there = place(p, k, n, partner)
        return remote(there, there, ds_.at[n, c], dr.at[n, c], partner)

    def each(fn):
        def one(k, _):
            for p in range(3):
                fn(p, k)
            return 0
        lax.fori_loop(0, 4, one, 0)
        fn(2, 4)

    for hop in range(3):
        each(lambda p, k: ici(p, k, hop, 0).start())
    each(lambda p, k: die(p, k, 0).start())
    own = pltpu.make_async_copy(mine.at[pl.ds(0, UNITS)], out.at[pl.ds(me * UNITS, UNITS)], lsem)
    own.start()

    def forward(n, hops):
        def fn(p, k):
            ici_arrival(p, k, n).wait_recv()
            for hop in hops:
                ici(p, k, hop, n).start()
            die(p, k, n).start()
        return fn

    each(forward(1, (1, 2)))
    each(forward(2, (2,)))
    each(forward(4, ()))
    each(forward(3, (2,)))
    each(forward(5, ()))
    each(forward(6, ()))
    each(forward(7, ()))
    for n in range(8):
        each(lambda p, k: die_arrival(p, k, n).wait_recv())
        each(lambda p, k: die(p, k, n).wait_send())
    for hop in range(3):
        for n in range(1 << hop):
            each(lambda p, k: ici(p, k, hop, n).wait_send())
    own.wait()


def all_gather(mine):
    dma = pltpu.SemaphoreType.DMA
    return pl.pallas_call(
        ag_kernel,
        out_shape=jax.ShapeDtypeStruct((NDEV * UNITS, 4, LANES), jnp.bfloat16),
        in_specs=[pl.BlockSpec(memory_space=pltpu.VMEM)],
        out_specs=pl.BlockSpec(memory_space=pl.ANY),
        scratch_shapes=[dma((8, AG_CHUNKS)), dma((8, AG_CHUNKS)), dma((8, AG_CHUNKS)), dma((8, AG_CHUNKS)), dma(())],
        compiler_params=pltpu.CompilerParams(collective_id=1, has_side_effects=True),
        name='all_gather',
    )(mine)


def solution(mesh):
    def local_step(grad_row, master, mom_first, mom_second, decay_mask, learn_rate):
        g, parts, _ = reduce_scatter(grad_row)
        p, w, m, v, norm = adam(learn_rate, parts, g, master, mom_first, mom_second, decay_mask)
        params = all_gather(p.reshape(ROWS_PAD // 4, 4, LANES))
        return params.reshape(-1), w.reshape(-1), m.reshape(-1), v.reshape(-1), norm[0, 0:1]

    return jax.shard_map(local_step, mesh=mesh, in_specs=(P('dp', None), P('dp'), P('dp'), P('dp'), P('dp'), P()), out_specs=(P(), P('dp'), P('dp'), P('dp'), P()), check_vma=False)
```

time: 1310 us -> 337 us (0.26)
  other arithmetic: 491 us -> 0 us
  blocking collectives: 351 us -> 0 us
  Pallas kernels: 0 us -> 315 us
  local copies, waits for them, and re-layouts: 236 us -> 20.6 us
  waiting for transfers between devices: 208 us -> 0 us
  between operations: 16.7 us -> 1.3 us
    pallas_call x0 -> x3, Pallas kernels: none -> 315 us  [the longest x1 200 us: reduce_scatter(): pl.pallas_call(rs_kernel, out_shape=(jax.ShapeDtypeStruct((ROWS_PAD, LANE...]
    all_to_all x1 -> x0, blocking collectives: 315 us -> none  [local_step(): received = lax.all_to_all(grad_parts, 'dp', 0, 0, tiled=True)]
    unnamed x4 -> x1, local copies, waits for them, and re-layouts: 235 us -> 19.4 us
    all_gather x1 -> x0, waiting for transfers between devices: 208 us -> none  [local_step(): params = lax.all_gather(new_master.astype(jnp.bfloat16), 'dp', tiled=True)]
    all_to_all x1 -> x0, other arithmetic: 166 us -> none  [local_step(): received = lax.all_to_all(grad_parts, 'dp', 0, 0, tiled=True)]
    all_gather x1 -> x0, other arithmetic: 166 us -> none  [local_step(): params = lax.all_gather(new_master.astype(jnp.bfloat16), 'dp', tiled=True)]
    reduce_sum x2 -> x0, other arithmetic: 150 us -> none  [the longest x1 148 us: local_step(): grad_mean = jnp.sum(received, axis=0, dtype=jnp.float32) / num_dev]
    psum x1 -> x0, blocking collectives: 36 us -> none  [local_step(): sq_total = lax.psum(jnp.sum(grad_mean * grad_mean), 'dp')]
  transfers between devices with their start and end apart: 1 -> 0, of which waited for: 1 -> 0; matrix products, arithmetic and copies ran while one was open for 0% -> 0% of each run, Pallas kernels for 0% -> 0%
where the time goes in v1:
time: 337 us
  Pallas kernels  315 us (93%)
  local copies, waits for them, and re-layouts  20.6 us (6%)
    pallas_call x1, Pallas kernels, reduce_scatter(): pl.pallas_call(rs_kernel, out_shape=(jax.ShapeDtypeStruct((ROWS_PAD, LANE...  200 us
    pallas_call x1, Pallas kernels, all_gather(): pl.pallas_call(ag_kernel, out_shape=jax.ShapeDtypeStruct((NDEV * UNITS, 4...  98.9 us
    unnamed x1, local copies, waits for them, and re-layouts  19.4 us
    pallas_call x1, Pallas kernels, adam(): pl.pallas_call(adam_kernel, grid=(CHUNKS,), out_shape=(jax.ShapeDtypeStru...  16.3 us

profile of v1, /device:TPU:0, one launch (start us, length us, event | category | flops | bytes accessed | tf_op | source)
XLA Modules:
  0.0 336.8 jit_solution(866132688841154750)
XLA Ops:
  1.3 199.8 %reduce_scatter.1 = (f32[6912,128]{1,0:T(8,128)}, f32[8,128]{1,0:T(8,128)}, bf16[96,1,73728]{2,1,0:T(2,128)(2,1)}) custom-call(bf16[1,14147584]{1,0:T(2,128)(2,1)} %grad.1), custom_call_target="tpu_custom_call" | custom-call | tf_op jit(solution)/shard_map/reduce_scatter/pallas_call | solution.py:282
  201.1 16.3 %adam.1 = (bf16[6912,128]{1,0:T(8,128)(2,1)}, f32[6908,128]{1,0:T(8,128)}, f32[6908,128]{1,0:T(8,128)}, f32[6908,128]{1,0:T(8,128)}, f32[8,128]{1,0:T(8,128)}) custom-call(f32[1]{0:T(128)S(6)} %copy.12.lr, f32[8,128]{1,0:T(8,128)} %get-tuple-element.12.parts, f32[6912,128]{1,0:T(8,128)} %get-tuple-element.13.g, f32[6908,128]{1,0:T(8,128)} %bitcast.11, ...), custom_call_target="tpu_custom_call" | custom-call | tf_op jit(solution)/shard_map/adam/pallas_call | solution.py:330
  217.3 1.2 slice.3
  218.5 98.9 %all_gather.1 = bf16[27632,4,128]{2,1,0:T(4,128)(2,1)} custom-call(bf16[1728,4,128]{2,1,0:T(4,128)(2,1)} %bitcast.15), custom_call_target="tpu_custom_call" | custom-call | tf_op jit(solution)/shard_map/all_gather/pallas_call | solution.py:421
  317.4 19.4 %copy.13 = bf16[14147584]{0:T(1024)(128)(2,1)} copy(bf16[14147584]{0:T(1024)(128)(2,1)} %bitcast.10) | data formatting | bytes 56590336

commit v2 on v1

--- a/solution.py
+++ b/solution.py
@@ -23,11 +23,7 @@
 NSLAB = CR // SLAB
 DEPTH = 4
 UNITS = ROWS // 4
-PART_UNIT0 = (0, 576, 1152)
-PART_COUNT = (4, 4, 5)
-PART_UNITS = (144, 144, 115)
-PART_BASE = (0, 4, 8)
-AG_CHUNKS = 13
+AG_UNITS = 144
 
 MESH = pl.DeviceIdType.MESH
 
@@ -281,7 +277,7 @@
     dma = pltpu.SemaphoreType.DMA
     return pl.pallas_call(
         rs_kernel,
-        out_shape=(jax.ShapeDtypeStruct((ROWS_PAD, LANES), f32), jax.ShapeDtypeStruct((8, LANES), f32), jax.ShapeDtypeStruct((96, 1, CW), jnp.bfloat16)),
+        out_shape=(pltpu.VMEM((ROWS_PAD, LANES), f32), pltpu.VMEM((8, LANES), f32), jax.ShapeDtypeStruct((96, 1, CW), jnp.bfloat16)),
         in_specs=[pl.BlockSpec(memory_space=pl.ANY)],
         out_specs=(pl.BlockSpec(memory_space=pltpu.VMEM), pl.BlockSpec(memory_space=pltpu.VMEM), pl.BlockSpec(memory_space=pl.ANY)),
         scratch_shapes=[
@@ -305,99 +301,128 @@
     )(grad)
 
 
-def adam_kernel(lr, parts, g, w, m, v, mask, p_out, w_out, m_out, v_out, norm_out):
-    norm = jnp.sqrt(jnp.sum(parts[...], keepdims=True))
-    norm_out[...] = jnp.broadcast_to(norm, norm_out.shape)
-    clip = jnp.minimum(1.0, 1.0 / (norm + CLIP_EPS))
-    h = g[...] * clip
-    m_new = BETA_FIRST * m[...] + (1.0 - BETA_FIRST) * h
-    v_new = BETA_SECOND * v[...] + (1.0 - BETA_SECOND) * h * h
+def adam_slab(lr, clip, g, w, m, v, mask):
+    h = g * clip
+    m_new = BETA_FIRST * m + (1.0 - BETA_FIRST) * h
+    v_new = BETA_SECOND * v + (1.0 - BETA_SECOND) * h * h
     step_dir = (m_new / (1.0 - BETA_FIRST ** ADAM_STEP)) / (jnp.sqrt(v_new / (1.0 - BETA_SECOND ** ADAM_STEP)) + ADAM_EPS)
-    old = w[...]
-    w_new = old - lr[0] * (step_dir + WEIGHT_DECAY * mask[...].astype(jnp.float32) * old)
-    w_out[...] = w_new
-    m_out[...] = m_new
-    v_out[...] = v_new
-    p_out[...] = w_new.astype(jnp.bfloat16)
-
-
-def adam(lr, parts, g, w, m, v, mask):
-    f32 = jnp.float32
-    block = pl.BlockSpec((CR, LANES), lambda i: (i, 0))
-    whole = pl.BlockSpec((8, LANES), lambda i: (0, 0))
-    flat = lambda a: a.reshape(ROWS, LANES)
-    state = jax.ShapeDtypeStruct((ROWS, LANES), f32)
-    return pl.pallas_call(
-        adam_kernel,
-        grid=(CHUNKS,),
-        out_shape=(jax.ShapeDtypeStruct((ROWS_PAD, LANES), jnp.bfloat16), state, state, state, jax.ShapeDtypeStruct((8, LANES), f32)),
-        in_specs=[pl.BlockSpec(memory_space=pltpu.SMEM), whole, block, block, block, block, block],
-        out_specs=(block, block, block, block, whole),
-        name='adam',
-    )(lr, parts, g, flat(w), flat(m), flat(v), flat(mask))
-
-
-def ag_kernel(mine, out, is_, ir, ds_, dr, lsem):
+    w_new = w - lr * (step_dir + WEIGHT_DECAY * mask.astype(jnp.float32) * w)
+    return w_new, m_new, v_new
+
+
+def ag_kernel(lr, parts, g, w_in, m_in, v_in, mask_in, w, m, v, norm_out, out, mask, is_, ir, ds_, dr, ld):
     me = lax.axis_index('dp')
     partner = me + 1 - 2 * (me % 2)
     barrier = pltpu.get_barrier_semaphore()
     near = [me + step_of(me, a) for a in range(3)]
     for other in near + [partner]:
         pl.semaphore_signal(barrier, inc=1, device_id=(other,), device_id_type=MESH)
-    pl.semaphore_wait(barrier, 4)
-
-    def place(p, k, n, dev=me):
+
+    def loads(q, size=CR):
+        start = q * CR
+        if not isinstance(start, int):
+            start = pl.multiple_of(start, 8)
+        rows = pl.ds(start, size)
+        pairs = ((w_in, w), (m_in, m), (v_in, v), (mask_in, mask))
+        return [pltpu.make_async_copy(a.at[rows], b.at[rows], ld.at[i, q]) for i, (a, b) in enumerate(pairs)]
+
+    def each(fn, first=0):
+        def one(k, _):
+            for p in range(3):
+                fn(p, k, AG_UNITS)
+            return 0
+        lax.fori_loop(first, 3, one, 0)
+        fn(0, 3, AG_UNITS)
+        fn(1, 3, AG_UNITS)
+        fn(2, 3, UNITS - 11 * AG_UNITS)
+
+    def start_loads(p, k, units):
+        for c in loads(4 * p + k, 4 * units):
+            c.start()
+
+    each(start_loads)
+
+    norm = jnp.sqrt(jnp.sum(parts[...], keepdims=True))
+    norm_out[...] = jnp.broadcast_to(norm, norm_out.shape)
+    clip = jnp.minimum(1.0, 1.0 / (norm + CLIP_EPS))
+
+    def place(p, k, units, n, dev=me):
         a = [p, (p + 1) % 3, (p + 2) % 3]
         block = dev
         for bit in range(3):
             if (n >> bit) & 1:
                 block = block + step_of(me, a[bit])
-        return out.at[pl.ds(block * UNITS + PART_UNIT0[p] + PART_UNITS[p] * k, PART_UNITS[p])]
-
-    def source(p, k, n):
-        if n == 0:
-            return mine.at[pl.ds(PART_UNIT0[p] + PART_UNITS[p] * k, PART_UNITS[p])]
-        return place(p, k, n)
-
-    def ici(p, k, hop, n):
+        return out.at[pl.ds(block * UNITS + AG_UNITS * (4 * p + k), units)]
+
+    def ici(p, k, units, hop, n):
         slot = n | (1 << hop)
-        c = PART_BASE[p] + k
-        return remote(source(p, k, n), place(p, k, n), is_.at[slot, c], ir.at[slot, c], near[(p + hop) % 3])
-
-    def ici_arrival(p, k, n):
+        c = 4 * p + k
+        here = place(p, k, units, n)
+        return remote(here, here, is_.at[slot, c], ir.at[slot, c], near[(p + hop) % 3])
+
+    def ici_arrival(p, k, units, n):
         hop = n.bit_length() - 1
-        c = PART_BASE[p] + k
-        return remote(place(p, k, n), place(p, k, n), is_.at[n, c], ir.at[n, c], near[(p + hop) % 3])
-
-    def die(p, k, n):
-        c = PART_BASE[p] + k
-        return remote(source(p, k, n), place(p, k, n), ds_.at[n, c], dr.at[n, c], partner)
-
-    def die_arrival(p, k, n):
-        c = PART_BASE[p] + k
-        there = place(p, k, n, partner)
+        c = 4 * p + k
+        here = place(p, k, units, n)
+        return remote(here, here, is_.at[n, c], ir.at[n, c], near[(p + hop) % 3])
+
+    def die(p, k, units, n):
+        c = 4 * p + k
+        here = place(p, k, units, n)
+        return remote(here, here, ds_.at[n, c], dr.at[n, c], partner)
+
+    def die_arrival(p, k, units, n):
+        c = 4 * p + k
+        there = place(p, k, units, n, partner)
         return remote(there, there, ds_.at[n, c], dr.at[n, c], partner)
 
-    def each(fn):
-        def one(k, _):
-            for p in range(3):
-                fn(p, k)
-            return 0
-        lax.fori_loop(0, 4, one, 0)
-        fn(2, 4)
-
-    for hop in range(3):
-        each(lambda p, k: ici(p, k, hop, 0).start())
-    each(lambda p, k: die(p, k, 0).start())
-    own = pltpu.make_async_copy(mine.at[pl.ds(0, UNITS)], out.at[pl.ds(me * UNITS, UNITS)], lsem)
-    own.start()
+    def update(p, k, units):
+        q = 4 * p + k
+        for c in loads(q, 4 * units):
+            c.wait()
+        rate = lr[0]
+
+        def slab(row0, n):
+            rows = pl.ds(row0, n)
+            w_new, m_new, v_new = adam_slab(rate, clip, g[rows, :], w[rows, :], m[rows, :], v[rows, :], mask[rows, :])
+            w[rows, :] = w_new
+            m[rows, :] = m_new
+            v[rows, :] = v_new
+            return w_new.astype(jnp.bfloat16).reshape(n // 4, 4, LANES)
+
+        whole = (4 * units) // SLAB
+
+        def one(i, _):
+            out[pl.ds(me * UNITS + q * AG_UNITS + i * (SLAB // 4), SLAB // 4)] = slab(pl.multiple_of(q * CR + i * SLAB, 8), SLAB)
+            return 0
+        lax.fori_loop(0, whole, one, 0)
+        rest = 4 * units - whole * SLAB
+        if rest:
+            out[pl.ds(me * UNITS + q * AG_UNITS + whole * (SLAB // 4), rest // 4)] = slab(q * CR + whole * SLAB, rest)
+
+    for p in range(3):
+        update(p, 0, AG_UNITS)
+        if p == 0:
+            pl.semaphore_wait(barrier, 4)
+        for hop in range(3):
+            ici(p, 0, AG_UNITS, hop, 0).start()
+        die(p, 0, AG_UNITS, 0).start()
+
+    def later(p, k, units):
+        update(p, k, units)
+        ici(p, k, units, 0, 0).start()
+
+    each(later, 1)
+    for hop in (1, 2):
+        each(lambda p, k, units: ici(p, k, units, hop, 0).start(), 1)
+    each(lambda p, k, units: die(p, k, units, 0).start(), 1)
 
     def forward(n, hops):
-        def fn(p, k):
-            ici_arrival(p, k, n).wait_recv()
+        def fn(p, k, units):
+            ici_arrival(p, k, units, n).wait_recv()
             for hop in hops:
-                ici(p, k, hop, n).start()
-            die(p, k, n).start()
+                ici(p, k, units, hop, n).start()
+            die(p, k, units, n).start()
         return fn
 
     each(forward(1, (1, 2)))
@@ -408,32 +433,66 @@
     each(forward(6, ()))
     each(forward(7, ()))
     for n in range(8):
-        each(lambda p, k: die_arrival(p, k, n).wait_recv())
-        each(lambda p, k: die(p, k, n).wait_send())
+        each(lambda p, k, units: die_arrival(p, k, units, n).wait_recv())
+        each(lambda p, k, units: die(p, k, units, n).wait_send())
     for hop in range(3):
         for n in range(1 << hop):
-            each(lambda p, k: ici(p, k, hop, n).wait_send())
-    own.wait()
-
-
-def all_gather(mine):
+            each(lambda p, k, units: ici(p, k, units, hop, n).wait_send())
+
+
+def adam_gather(lr, parts, g, w, m, v, mask):
+    f32 = jnp.float32
     dma = pltpu.SemaphoreType.DMA
+    flat = lambda a: pltpu.with_memory_space_constraint(a.reshape(ROWS, LANES), pltpu.HBM)
+    hbm = pl.BlockSpec(memory_space=pl.ANY)
+    vmem = pl.BlockSpec(memory_space=pltpu.VMEM)
+    state = pltpu.VMEM((ROWS, LANES), f32)
     return pl.pallas_call(
         ag_kernel,
-        out_shape=jax.ShapeDtypeStruct((NDEV * UNITS, 4, LANES), jnp.bfloat16),
-        in_specs=[pl.BlockSpec(memory_space=pltpu.VMEM)],
-        out_specs=pl.BlockSpec(memory_space=pl.ANY),
-        scratch_shapes=[dma((8, AG_CHUNKS)), dma((8, AG_CHUNKS)), dma((8, AG_CHUNKS)), dma((8, AG_CHUNKS)), dma(())],
-        compiler_params=pltpu.CompilerParams(collective_id=1, has_side_effects=True),
-        name='all_gather',
-    )(mine)
+        out_shape=(state, state, state, jax.ShapeDtypeStruct((8, LANES), f32), pltpu.VMEM((NDEV * UNITS, 4, LANES), jnp.bfloat16)),
+        in_specs=[pl.BlockSpec(memory_space=pltpu.SMEM), vmem, vmem, hbm, hbm, hbm, hbm],
+        out_specs=(vmem, vmem, vmem, vmem, vmem),
+        scratch_shapes=[pltpu.VMEM((ROWS, LANES), jnp.int32), dma((8, CHUNKS)), dma((8, CHUNKS)), dma((8, CHUNKS)), dma((8, CHUNKS)), dma((4, CHUNKS))],
+        compiler_params=pltpu.CompilerParams(collective_id=1, has_side_effects=True, vmem_limit_bytes=8 * 1024 * 1024),
+        name='adam_gather',
+    )(lr, pltpu.with_memory_space_constraint(parts, pltpu.VMEM), pltpu.with_memory_space_constraint(g, pltpu.VMEM), flat(w), flat(m), flat(v), flat(mask))
+
+
+PUBLISH_PIECES = 8
+
+
+def publish_kernel(p_in, w_in, m_in, v_in, n_in, p_out, w_out, m_out, v_out, n_out, big, small):
+    size = NDEV * UNITS // PUBLISH_PIECES
+    copies = [pltpu.make_async_copy(p_in.at[pl.ds(i * size, size)], p_out.at[pl.ds(i * size, size)], big.at[i]) for i in range(PUBLISH_PIECES)]
+    copies += [pltpu.make_async_copy(a, b, small.at[i]) for i, (a, b) in enumerate(((w_in, w_out), (m_in, m_out), (v_in, v_out)))]
+    for c in copies:
+        c.start()
+    n_out[...] = n_in[0, 0:1]
+    for c in copies:
+        c.wait()
+
+
+def publish(arrays, norm):
+    dma = pltpu.SemaphoreType.DMA
+    vmem = pl.BlockSpec(memory_space=pltpu.VMEM)
+    hbm = pl.BlockSpec(memory_space=pl.ANY)
+    arrays = [pltpu.with_memory_space_constraint(a, pltpu.VMEM) for a in arrays]
+    return pl.pallas_call(
+        publish_kernel,
+        out_shape=[jax.ShapeDtypeStruct(a.shape, a.dtype) for a in arrays] + [jax.ShapeDtypeStruct((1,), jnp.float32)],
+        in_specs=[vmem] * 5,
+        out_specs=[hbm] * 4 + [vmem],
+        scratch_shapes=[dma((PUBLISH_PIECES,)), dma((3,))],
+        compiler_params=pltpu.CompilerParams(vmem_limit_bytes=1024 * 1024),
+        name='publish',
+    )(*arrays, norm)
 
 
 def solution(mesh):
     def local_step(grad_row, master, mom_first, mom_second, decay_mask, learn_rate):
         g, parts, _ = reduce_scatter(grad_row)
-        p, w, m, v, norm = adam(learn_rate, parts, g, master, mom_first, mom_second, decay_mask)
-        params = all_gather(p.reshape(ROWS_PAD // 4, 4, LANES))
-        return params.reshape(-1), w.reshape(-1), m.reshape(-1), v.reshape(-1), norm[0, 0:1]
+        w, m, v, norm, params = adam_gather(learn_rate, parts, g, master, mom_first, mom_second, decay_mask)
+        params, w, m, v, norm = publish([params, w, m, v], norm)
+        return params.reshape(-1), w.reshape(-1), m.reshape(-1), v.reshape(-1), norm
 
     return jax.shard_map(local_step, mesh=mesh, in_specs=(P('dp', None), P('dp'), P('dp'), P('dp'), P('dp'), P()), out_specs=(P(), P('dp'), P('dp'), P('dp'), P()), check_vma=False)

time: 337 us -> 310 us (0.920)
  local copies, waits for them, and re-layouts: 20.6 us -> 0 us
  Pallas kernels: 315 us -> 309 us
    unnamed x1 -> x0, local copies, waits for them, and re-layouts: 19.4 us -> none
    pallas_call x3, Pallas kernels: 315 us -> 309 us  [the longest x1 198 us: reduce_scatter(): pl.pallas_call(rs_kernel, out_shape=(pltpu.VMEM((ROWS_PAD, LANES), f32),...]
where the time goes in v2:
time: 310 us
  Pallas kernels  309 us (100%)
    pallas_call x1, Pallas kernels, reduce_scatter(): pl.pallas_call(rs_kernel, out_shape=(pltpu.VMEM((ROWS_PAD, LANES), f32),...  198 us
    pallas_call x1, Pallas kernels, adam_gather(): pl.pallas_call(ag_kernel, out_shape=(state, state, state, jax.ShapeDtypeS...  97.8 us
    pallas_call x1, Pallas kernels, publish(): pl.pallas_call(publish_kernel, out_shape=[jax.ShapeDtypeStruct(a.shape, a...  13.2 us

profile of v2, /device:TPU:0, one launch (start us, length us, event | category | flops | bytes accessed | tf_op | source)
XLA Modules:
  0.0 310.2 jit_solution(3541571633793582381)
XLA Ops:
  1.3 197.9 %reduce_scatter.1 = (f32[6912,128]{1,0:T(8,128)S(1)}, f32[8,128]{1,0:T(8,128)S(1)}, bf16[96,1,73728]{2,1,0:T(2,128)(2,1)}) custom-call(bf16[1,14147584]{1,0:T(2,128)(2,1)} %grad.1), custom_call_target="tpu_custom_call" | custom-call | tf_op jit(solution)/shard_map/reduce_scatter/pallas_call | solution.py:278
  199.2 97.8 %adam_gather.1 = (f32[6908,128]{1,0:T(8,128)S(1)}, f32[6908,128]{1,0:T(8,128)S(1)}, f32[6908,128]{1,0:T(8,128)S(1)}, f32[8,128]{1,0:T(8,128)S(1)}, bf16[27632,4,128]{2,1,0:T(4,128)(2,1)S(1)}) custom-call(f32[1]{0:T(128)S(6)} %copy.11.lr, f32[8,128]{1,0:T(8,128)S(1)} %get-tuple-element.17.parts, f32[6912,128]{1,0:T(8,128)S(1)} %get-tuple-element.18.g, ...), custom_call_target="tpu_custom_call" | custom-call | tf_op jit(solution)/shard_map/adam_gather/pallas_call | solution.py:450
  297.0 13.2 %publish.1 = (bf16[27632,4,128]{2,1,0:T(4,128)(2,1)}, f32[6908,128]{1,0:T(8,128)}, f32[6908,128]{1,0:T(8,128)}, f32[6908,128]{1,0:T(8,128)}, f32[1]{0:T(128)}) custom-call(bf16[27632,4,128]{2,1,0:T(4,128)(2,1)S(1)} %get-tuple-element.19.p_in, f32[6908,128]{1,0:T(8,128)S(1)} %get-tuple-element.20.w_in, f32[6908,128]{1,0:T(8,128)S(1)} %get-tuple-element.21.m_in, ...), custom_call_target="tpu_custom_call" | custom-call | tf_op jit(solution)/shard_map/publish/pallas_call | solution.py:480

commit v3 on v0

v3 whole, which is shorter than its diff:
```python
import jax
import jax.numpy as jnp
from jax import lax
from jax.experimental import pallas as pl
from jax.experimental.pallas import tpu as pltpu
from jax.sharding import PartitionSpec as P

BETA_FIRST = 0.9
BETA_SECOND = 0.95
ADAM_EPS = 1e-8
CLIP_EPS = 1e-6
WEIGHT_DECAY = 0.1
ADAM_STEP = 10

NDEV = 16
LANES = 128
ROWS = 6908
ROWS_PAD = 6912
CHUNKS = 12
CR = 576
CW = CR * LANES
SLAB = 72
NSLAB = CR // SLAB
DEPTH = 4
SENDS = 24
UNITS = ROWS // 4
LATE = 12
AG_UNITS = 144

MESH = pl.DeviceIdType.MESH


def weight(axis):
    return 2 + axis + axis * axis


def step_of(me, axis):
    w = weight(axis)
    return (1 - 2 * ((me // w) % 2)) * w


def chunk_row(q):
    return CR * q - 4 * (q // (CHUNKS - 1))


def remote(src, dst, ssem, rsem, dev):
    return pltpu.make_async_remote_copy(src_ref=src, dst_ref=dst, send_sem=ssem, recv_sem=rsem, device_id=(dev,), device_id_type=MESH)


def adam_slab(lr, clip, g, w, m, v, mask):
    h = g * clip
    m_new = BETA_FIRST * m + (1.0 - BETA_FIRST) * h
    v_new = BETA_SECOND * v + (1.0 - BETA_SECOND) * h * h
    step_dir = (m_new / (1.0 - BETA_FIRST ** ADAM_STEP)) / (jnp.sqrt(v_new / (1.0 - BETA_SECOND ** ADAM_STEP)) + ADAM_EPS)
    w_new = w - lr * (step_dir + WEIGHT_DECAY * mask.astype(jnp.float32) * w)
    return w_new, m_new, v_new


def step_kernel(lr, grad, w_in, m_in, v_in, mask_in, w, m, v, norm_out, out, prow, r1, r2,
                own, par, st1, st2, early, mask, sb, r3, acc, nrm,
                psend, precv, sent, s1r, s2r, s3r, ns, nr, lo, lp, l1, l2, ld, is_, ir, ds_, dr):
    me = lax.axis_index('dp')
    partner = me + 1 - 2 * (me % 2)
    near = [me + step_of(me, a) for a in range(3)]

    def decode(phase, t):
        p = t % 3
        j = t // 3
        if phase == 1:
            o1, o2, o3, k = 1, j % 2, (j // 2) % 2, j // 4
        elif phase == 2:
            o1, o2, o3, k = 0, 1, j % 2, j // 2
        elif phase == 3:
            o1, o2, o3, k = 0, 0, 1, j
        else:
            o1, o2, o3, k = 0, 0, 0, j
        a1, a2, a3 = p, (p + 1) % 3, (p + 2) % 3
        shift = o1 * step_of(me, a1) + o2 * step_of(me, a2) + o3 * step_of(me, a3)
        return p, j, k, a1, a2, a3, shift, 4 * p + k

    base_of = {1: 0, 2: 48, 3: 72, 4: 84}
    count_of = {1: 48, 2: 24, 3: 12, 4: 12}

    def grad_slice(block, q):
        start = pl.multiple_of((block * ROWS + chunk_row(q)) * LANES, LANES)
        return grad.at[:, pl.ds(start, CW)]

    def early_copy(t):
        _, _, _, _, _, _, shift, q = decode(1, t)
        return remote(grad_slice(partner + shift, q), early.at[t], psend, precv.at[LATE + 1 + t], partner)

    def partner_copy(phase, t):
        _, _, _, _, _, _, shift, q = decode(phase, t)
        group = t // DEPTH if phase == 1 else LATE
        return remote(grad_slice(partner + shift, q), prow.at[base_of[phase] + t], psend, precv.at[group], partner)

    def rows_here(first, count, group):
        rows = prow.at[pl.ds(first, count)]
        return remote(rows, rows, psend, precv.at[group], partner)

    def own_load(phase, t):
        _, _, _, _, _, _, shift, q = decode(phase, t)
        slot = t % DEPTH
        return pltpu.make_async_copy(grad_slice(me + shift, q), own.at[slot], lo.at[slot])

    def s1_copy(t):
        p, j, k, *_ = decode(1, t)
        return remote(sb.at[t % SENDS], r1.at[(4 * p + k) * 4 + j % 4], sent.at[t % SENDS], s1r.at[4 * p + k], me + step_of(me, p))

    def s2_copy(t):
        p, j, k, *_ = decode(2, t)
        return remote(sb.at[t % SENDS], r2.at[(4 * p + k) * 2 + j % 2], sent.at[t % SENDS], s2r.at[4 * p + k], me + step_of(me, (p + 1) % 3))

    def s3_copy(t):
        p, j, k, *_ = decode(3, t)
        return remote(sb.at[t % SENDS], r3.at[t], sent.at[t % SENDS], s3r.at[t], me + step_of(me, (p + 2) % 3))

    def s1_group(q):
        rows = r1.at[pl.ds(q * 4, 4)]
        return remote(rows, rows, sent.at[0], s1r.at[q], partner)

    def s2_group(q):
        rows = r2.at[pl.ds(q * 2, 2)]
        return remote(rows, rows, sent.at[0], s2r.at[q], partner)

    def r1_at(p, k, o2, o3):
        return (4 * p + k) * 4 + o3 * 2 + o2

    def r2_at(p, k, o3):
        return (4 * p + k) * 2 + o3

    def sources(phase, t):
        p, j, k, *_ = decode(phase, t)
        if phase == 2:
            return r1_at(p, k, 1, j % 2), None
        if phase == 3:
            return r1_at(p, k, 0, 1), r2_at(p, k, 1)
        return r1_at(p, k, 0, 0), r2_at(p, k, 0)

    def loads(phase, t):
        slot = t % DEPTH
        copies = [own_load(phase, t), pltpu.make_async_copy(prow.at[base_of[phase] + t], par.at[slot], lp.at[slot])]
        if phase > 1:
            i1, i2 = sources(phase, t)
            copies.append(pltpu.make_async_copy(r1.at[i1], st1.at[slot], l1.at[slot]))
            if phase > 2:
                copies.append(pltpu.make_async_copy(r2.at[i2], st2.at[slot], l2.at[slot]))
        return copies

    def start_loads(phase, t):
        p, j, k, *_ = decode(phase, t)
        if phase == 1:
            if isinstance(t, int):
                if t % DEPTH == 0:
                    rows_here(t, DEPTH, t // DEPTH).wait_recv()
            else:
                @pl.when(t % DEPTH == 0)
                def _():
                    rows_here(t, DEPTH, t // DEPTH).wait_recv()
        elif phase == 2:
            if isinstance(j, int):
                if j % 2 == 0:
                    s1_group(4 * p + k).wait_recv()
            else:
                @pl.when(j % 2 == 0)
                def _():
                    s1_group(4 * p + k).wait_recv()
        elif phase == 3:
            s2_group(4 * p + k).wait_recv()
        for c in loads(phase, t):
            c.start()

    def chip_sum(slot, i, rows_of=None):
        rows_of = par if rows_of is None else rows_of
        cols = pl.ds(pl.multiple_of(i * (SLAB * LANES), SLAB * LANES), SLAB * LANES)
        total = own[slot, :, cols].astype(jnp.float32) + rows_of[slot, :, cols].astype(jnp.float32)
        return total.reshape(SLAB, LANES)

    def slabs(fn):
        def one(i, _):
            fn(i, pl.ds(pl.multiple_of(i * SLAB, SLAB), SLAB))
            return 0
        lax.fori_loop(0, NSLAB, one, 0)

    def loop(lo_t, hi_t, fn):
        def one(t, _):
            fn(t)
            return 0
        lax.fori_loop(lo_t, hi_t, one, 0)

    def run_phase(phase, body, first=0):
        n = count_of[phase]
        for t in range(DEPTH - 1):
            start_loads(phase, first + t)

        def one(t):
            @pl.when(t + DEPTH - 1 < n)
            def _():
                start_loads(phase, t + DEPTH - 1)
            for c in loads(phase, t):
                c.wait()
            body(t)
        loop(first, n, one)

    barrier = pltpu.get_barrier_semaphore()
    for other in [partner] + near:
        pl.semaphore_signal(barrier, inc=1, device_id=(other,), device_id_type=MESH)
    for t in range(DEPTH):
        own_load(1, t).start()
    pl.semaphore_wait(barrier, 4)

    for t in range(DEPTH):
        early_copy(t).start()
    loop(DEPTH, 16, lambda t: partner_copy(1, t).start())
    for t in range(DEPTH):
        own_load(1, t).wait()
        early_copy(t).wait_recv()

        def fn(i, rows):
            sb[t, rows, :] = chip_sum(t, i, early)
        slabs(fn)
        s1_copy(t).start()
    loop(16, 48, lambda t: partner_copy(1, t).start())

    def phase1(t):
        @pl.when(t >= SENDS)
        def _():
            s1_copy(t - SENDS).wait_send()
        slot = t % DEPTH

        def fn(i, rows):
            sb[t % SENDS, rows, :] = chip_sum(slot, i)
        slabs(fn)
        s1_copy(t).start()

    def phase2(t):
        s1_copy(t + SENDS).wait_send()
        slot = t % DEPTH

        def fn(i, rows):
            sb[t % SENDS, rows, :] = chip_sum(slot, i) + st1[slot, rows, :]
        slabs(fn)
        s2_copy(t).start()

    def phase3(t):
        s2_copy(t).wait_send()
        slot = t % DEPTH

        def fn(i, rows):
            sb[t % SENDS, rows, :] = chip_sum(slot, i) + st1[slot, rows, :] + st2[slot, rows, :]
        slabs(fn)
        s3_copy(t).start()

    acc[...] = jnp.zeros_like(acc)

    def phase4(t):
        slot = t % DEPTH
        p, j, k, *_ = decode(4, t)
        skip = 4 * ((4 * p + k) // (CHUNKS - 1))
        s3_copy(t).wait_recv()

        def fn(i, rows):
            g = (chip_sum(slot, i) + st1[slot, rows, :] + st2[slot, rows, :] + r3[t, rows, :]) * (1.0 / NDEV)
            r3[t, rows, :] = g
            row = lax.broadcasted_iota(jnp.int32, (SLAB, LANES), 0) + i * SLAB
            acc[...] += jnp.sum(jnp.where(row < skip, 0.0, g * g).reshape(SLAB // 8, 8, LANES), axis=0)
        slabs(fn)

    run_phase(1, phase1, DEPTH)
    for phase in (2, 3, 4):
        loop(0, count_of[phase], lambda t, phase=phase: partner_copy(phase, t).start())
    rows_here(48, 48, LATE).wait_recv()

    states = [pltpu.make_async_copy(a, b, ld.at[i]) for i, (a, b) in enumerate(((w_in, w), (m_in, m), (v_in, v), (mask_in, mask)))]
    for c in states:
        c.start()
    run_phase(2, phase2)
    for c in states:
        c.wait()
    rows_here(DEPTH, 96 - DEPTH, LATE).wait_send()
    remote(early, early, psend, precv.at[0], partner).wait_send()
    run_phase(3, phase3)
    loop(12, 24, lambda t: s2_copy(t).wait_send())
    run_phase(4, phase4)

    nrm[me] = acc[...]

    def norm_copy(i):
        return remote(acc, nrm.at[me], ns, nr, lax.rem(me + i, NDEV))

    others = nrm.at[pl.ds(0, NDEV - 1)]
    all_norms = remote(others, others, ns, nr, partner)

    loop(1, NDEV, lambda i: norm_copy(i).start())
    loop(0, 12, lambda t: s3_copy(t).wait_send())
    all_norms.wait_recv()
    total = nrm[0]
    for i in range(1, NDEV):
        total = total + nrm[i]
    norm = jnp.sqrt(jnp.sum(total, keepdims=True))
    norm_out[...] = jnp.broadcast_to(norm, norm_out.shape)
    clip = jnp.minimum(1.0, 1.0 / (norm + CLIP_EPS))
    rate = lr[0]

    def each(fn, first=0):
        def one(k, _):
            for p in range(3):
                fn(p, k, AG_UNITS)
            return 0
        lax.fori_loop(first, 3, one, 0)
        fn(0, 3, AG_UNITS)
        fn(1, 3, AG_UNITS)
        fn(2, 3, UNITS - 11 * AG_UNITS)

    def block_of(p, n):
        a = [p, (p + 1) % 3, (p + 2) % 3]
        block = me
        for bit in range(3):
            if (n >> bit) & 1:
                block = block + step_of(me, a[bit])
        return block

    def place(p, k, units, n):
        return out.at[pl.ds(block_of(p, n) * UNITS + AG_UNITS * (4 * p + k), units)]

    def place_part(p, n):
        units = 4 * AG_UNITS if p < 2 else UNITS - 8 * AG_UNITS
        return out.at[pl.ds(block_of(p, n) * UNITS + 4 * AG_UNITS * p, units)]

    def ir_index(p, k, n):
        if n in (4, 5, 6):
            return 48 + 3 * (n - 4) + p
        return 12 * (n if n < 4 else 0) + 4 * p + k

    def ici(p, k, units, hop, n):
        here = place(p, k, units, n)
        return remote(here, here, is_, ir.at[ir_index(p, k, n | (1 << hop))], near[(p + hop) % 3])

    def ici_arrival(p, k, units, n):
        here = place(p, k, units, n)
        return remote(here, here, is_, ir.at[ir_index(p, k, n)], partner)

    def part_arrival(p, n):
        here = place_part(p, n)
        return remote(here, here, is_, ir.at[ir_index(p, 0, n)], partner)

    def die(here):
        return remote(here, here, ds_, dr, partner)

    def update(p, k, units):
        q = 4 * p + k
        t = 3 * k + p
        short = units != AG_UNITS

        def slab(row0, n):
            rows = pl.ds(row0 + q * CR, n)
            src = pl.ds(row0 + 4, n) if short else pl.ds(row0, n)
            w_new, m_new, v_new = adam_slab(rate, clip, r3[t, src, :], w[rows, :], m[rows, :], v[rows, :], mask[rows, :])
            w[rows, :] = w_new
            m[rows, :] = m_new
            v[rows, :] = v_new
            return w_new.astype(jnp.bfloat16).reshape(n // 4, 4, LANES)

        base = me * UNITS + q * AG_UNITS
        whole = (4 * units) // SLAB
        if short:
            for i in range(whole):
                out[pl.ds(base + i * (SLAB // 4), SLAB // 4)] = slab(i * SLAB, SLAB)
            rest = 4 * units - whole * SLAB
            out[pl.ds(base + whole * (SLAB // 4), rest // 4)] = slab(whole * SLAB, rest)
        else:
            def one(i, _):
                out[pl.ds(base + i * (SLAB // 4), SLAB // 4)] = slab(pl.multiple_of(i * SLAB, SLAB), SLAB)
                return 0
            lax.fori_loop(0, whole, one, 0)

    for p in range(3):
        update(p, 0, AG_UNITS)
        for hop in range(3):
            ici(p, 0, AG_UNITS, hop, 0).start()

    def later(p, k, units):
        update(p, k, units)
        ici(p, k, units, 0, 0).start()

    each(later, 1)
    for hop in (1, 2):
        each(lambda p, k, units: ici(p, k, units, hop, 0).start(), 1)
    die(out.at[pl.ds(me * UNITS, UNITS)]).start()
    all_norms.wait_send()

    def forward(n, hops):
        def fn(p, k, units):
            ici_arrival(p, k, units, n).wait_recv()
            for hop in hops:
                ici(p, k, units, hop, n).start()
            die(place(p, k, units, n)).start()
        return fn

    def forward_part(n):
        for p in range(3):
            part_arrival(p, n).wait_recv()
            die(place_part(p, n)).start()

    each(forward(1, (1, 2)))
    each(forward(2, (2,)))
    each(forward(3, (2,)))
    forward_part(4)
    forward_part(5)
    forward_part(6)
    each(forward(7, ()))
    sends = out.at[pl.ds(0, 7 * UNITS)]
    remote(sends, sends, is_, ir.at[0], partner).wait_send()
    half = out.at[pl.ds(0, 8 * UNITS)]
    die(half).wait_send()
    die(half).wait_recv()


def step(lr, grad, w, m, v, mask):
    f32, bf16 = jnp.float32, jnp.bfloat16
    dma = pltpu.SemaphoreType.DMA
    flat = lambda a: pltpu.with_memory_space_constraint(a.reshape(ROWS, LANES), pltpu.HBM)
    hbm = pl.BlockSpec(memory_space=pl.ANY)
    vmem = pl.BlockSpec(memory_space=pltpu.VMEM)
    state = pltpu.VMEM((ROWS, LANES), f32)
    return pl.pallas_call(
        step_kernel,
        out_shape=(
            state, state, state, pltpu.VMEM((8, LANES), f32),
            pltpu.VMEM((NDEV * UNITS, 4, LANES), bf16),
            pltpu.HBM((96, 1, CW), bf16), pltpu.HBM((48, CR, LANES), f32), pltpu.HBM((24, CR, LANES), f32),
        ),
        in_specs=[pl.BlockSpec(memory_space=pltpu.SMEM)] + [hbm] * 5,
        out_specs=(vmem, vmem, vmem, vmem, vmem, hbm, hbm, hbm),
        scratch_shapes=[
            pltpu.VMEM((DEPTH, 1, CW), bf16),
            pltpu.VMEM((DEPTH, 1, CW), bf16),
            pltpu.VMEM((DEPTH, CR, LANES), f32),
            pltpu.VMEM((DEPTH, CR, LANES), f32),
            pltpu.VMEM((DEPTH, 1, CW), bf16),
            pltpu.VMEM((ROWS, LANES), jnp.int32),
            pltpu.VMEM((SENDS, CR, LANES), f32),
            pltpu.VMEM((12, CR, LANES), f32),
            pltpu.VMEM((8, LANES), f32),
            pltpu.VMEM((NDEV, 8, LANES), f32),
            dma(()), dma((LATE + 1 + DEPTH,)), dma((SENDS,)),
            dma((12,)), dma((12,)), dma((12,)),
            dma(()), dma(()),
            dma((DEPTH,)), dma((DEPTH,)), dma((DEPTH,)), dma((DEPTH,)),
            dma((4,)),
            dma(()), dma((57,)), dma(()), dma(()),
        ],
        compiler_params=pltpu.CompilerParams(collective_id=0, has_side_effects=True, vmem_limit_bytes=22 * 1024 * 1024),
        name='step',
    )(lr, grad, flat(w), flat(m), flat(v), flat(mask))


PUBLISH_PIECES = 8


def publish_kernel(p_in, w_in, m_in, v_in, n_in, p_out, w_out, m_out, v_out, n_out, big, small):
    size = NDEV * UNITS // PUBLISH_PIECES
    copies = [pltpu.make_async_copy(p_in.at[pl.ds(i * size, size)], p_out.at[pl.ds(i * size, size)], big.at[i]) for i in range(PUBLISH_PIECES)]
    copies += [pltpu.make_async_copy(a, b, small.at[i]) for i, (a, b) in enumerate(((w_in, w_out), (m_in, m_out), (v_in, v_out)))]
    for c in copies:
        c.start()
    n_out[...] = n_in[0, 0:1]
    for c in copies:
        c.wait()


def publish(arrays, norm):
    dma = pltpu.SemaphoreType.DMA
    vmem = pl.BlockSpec(memory_space=pltpu.VMEM)
    hbm = pl.BlockSpec(memory_space=pl.ANY)
    arrays = [pltpu.with_memory_space_constraint(a, pltpu.VMEM) for a in arrays]
    norm = pltpu.with_memory_space_constraint(norm, pltpu.VMEM)
    return pl.pallas_call(
        publish_kernel,
        out_shape=[jax.ShapeDtypeStruct(a.shape, a.dtype) for a in arrays] + [jax.ShapeDtypeStruct((1,), jnp.float32)],
        in_specs=[vmem] * 5,
        out_specs=[hbm] * 4 + [vmem],
        scratch_shapes=[dma((PUBLISH_PIECES,)), dma((3,))],
        compiler_params=pltpu.CompilerParams(vmem_limit_bytes=1024 * 1024),
        name='publish',
    )(*arrays, norm)


def solution(mesh):
    def local_step(grad_row, master, mom_first, mom_second, decay_mask, learn_rate):
        w, m, v, norm, params, *_ = step(learn_rate, grad_row, master, mom_first, mom_second, decay_mask)
        params, w, m, v, norm = publish([params, w, m, v], norm)
        return params.reshape(-1), w.reshape(-1), m.reshape(-1), v.reshape(-1), norm

    return jax.shard_map(local_step, mesh=mesh, in_specs=(P('dp', None), P('dp'), P('dp'), P('dp'), P('dp'), P()), out_specs=(P(), P('dp'), P('dp'), P('dp'), P()), check_vma=False)
```

time: 1310 us -> 298 us (0.23)
  other arithmetic: 491 us -> 0 us
  blocking collectives: 351 us -> 0 us
  Pallas kernels: 0 us -> 297 us
  local copies, waits for them, and re-layouts: 236 us -> 0 us
  waiting for transfers between devices: 208 us -> 0 us
  between operations: 16.7 us -> 1.29 us
    all_to_all x1 -> x0, blocking collectives: 315 us -> none  [local_step(): received = lax.all_to_all(grad_parts, 'dp', 0, 0, tiled=True)]
    pallas_call x0 -> x2, Pallas kernels: none -> 297 us  [the longest x1 284 us: step(): pl.pallas_call(step_kernel, out_shape=(state, state, state, pltpu.VMEM((8...]
    unnamed x4 -> x0, local copies, waits for them, and re-layouts: 235 us -> none
    all_gather x1 -> x0, waiting for transfers between devices: 208 us -> none  [local_step(): params = lax.all_gather(new_master.astype(jnp.bfloat16), 'dp', tiled=True)]
    all_to_all x1 -> x0, other arithmetic: 166 us -> none  [local_step(): received = lax.all_to_all(grad_parts, 'dp', 0, 0, tiled=True)]
    all_gather x1 -> x0, other arithmetic: 166 us -> none  [local_step(): params = lax.all_gather(new_master.astype(jnp.bfloat16), 'dp', tiled=True)]
    reduce_sum x2 -> x0, other arithmetic: 150 us -> none  [the longest x1 148 us: local_step(): grad_mean = jnp.sum(received, axis=0, dtype=jnp.float32) / num_dev]
    psum x1 -> x0, blocking collectives: 36 us -> none  [local_step(): sq_total = lax.psum(jnp.sum(grad_mean * grad_mean), 'dp')]
  transfers between devices with their start and end apart: 1 -> 0, of which waited for: 1 -> 0; matrix products, arithmetic and copies ran while one was open for 0% -> 0% of each run, Pallas kernels for 0% -> 0%
where the time goes in v3:
time: 298 us
  Pallas kernels  297 us (100%)
    pallas_call x1, Pallas kernels, step(): pl.pallas_call(step_kernel, out_shape=(state, state, state, pltpu.VMEM((8...  284 us
    pallas_call x1, Pallas kernels, publish(): pl.pallas_call(publish_kernel, out_shape=[jax.ShapeDtypeStruct(a.shape, a...  13.2 us

profile of v3, /device:TPU:0, one launch (start us, length us, event | category | flops | bytes accessed | tf_op | source)
XLA Modules:
  0.0 298.1 jit_solution(10549445735715756962)
XLA Ops:
  1.3 283.6 %step.1 = (f32[6908,128]{1,0:T(8,128)S(1)}, f32[6908,128]{1,0:T(8,128)S(1)}, f32[6908,128]{1,0:T(8,128)S(1)}, f32[8,128]{1,0:T(8,128)S(1)}, bf16[27632,4,128]{2,...) custom-call(f32[1]{0:T(128)S(6)} %copy.11.lr, ...), custom_call_target="tpu_custom_call" | custom-call | tf_op jit(solution)/shard_map/step/pallas_call | solution.py:426
  284.9 13.2 %publish.1 = (bf16[27632,4,128]{2,1,0:T(4,128)(2,1)}, f32[6908,128]{1,0:T(8,128)}, f32[6908,128]{1,0:T(8,128)}, f32[6908,128]{1,0:T(8,128)}, f32[1]{0:T(128)}) custom-call(bf16[27632,4,128]{2,1,0:T(4,128)(2,1)S(1)} %get-tuple-element.15.p_in, f32[6908,128]{1,0:T(8,128)S(1)} %get-tuple-element.16.w_in, f32[6908,128]{1,0:T(8,128)S(1)} %get-tuple-element.17.m_in, ...), custom_call_target="tpu_custom_call" | custom-call | tf_op jit(solution)/shard_map/publish/pallas_call | solution.py:478

commit v4 on v3

v4 whole, which is shorter than its diff:
```python
import jax
import jax.numpy as jnp
from jax import lax
from jax.experimental import pallas as pl
from jax.experimental.pallas import tpu as pltpu
from jax.sharding import PartitionSpec as P

BETA_FIRST = 0.9
BETA_SECOND = 0.95
ADAM_EPS = 1e-8
CLIP_EPS = 1e-6
WEIGHT_DECAY = 0.1
ADAM_STEP = 10

NDEV = 16
LANES = 128
ROWS = 6908
ROWS_PAD = 6912
CHUNKS = 12
CR = 576
CW = CR * LANES
SLAB = 72
NSLAB = CR // SLAB
DEPTH = 4
GROUPS = 6
UNITS = ROWS // 4
LATE = 12
AG_UNITS = 144

MESH = pl.DeviceIdType.MESH


def weight(axis):
    return 2 + axis + axis * axis


def step_of(me, axis):
    w = weight(axis)
    return (1 - 2 * ((me // w) % 2)) * w


def chunk_row(q):
    return CR * q - 4 * (q // (CHUNKS - 1))


def remote(src, dst, ssem, rsem, dev):
    return pltpu.make_async_remote_copy(src_ref=src, dst_ref=dst, send_sem=ssem, recv_sem=rsem, device_id=(dev,), device_id_type=MESH)


def adam_slab(lr, clip, g, w, m, v, mask):
    h = g * clip
    m_new = BETA_FIRST * m + (1.0 - BETA_FIRST) * h
    v_new = BETA_SECOND * v + (1.0 - BETA_SECOND) * h * h
    step_dir = (m_new / (1.0 - BETA_FIRST ** ADAM_STEP)) / (jnp.sqrt(v_new / (1.0 - BETA_SECOND ** ADAM_STEP)) + ADAM_EPS)
    w_new = w - lr * (step_dir + WEIGHT_DECAY * mask.astype(jnp.float32) * w)
    return w_new, m_new, v_new


def step_kernel(lr_in, grad, w_in, m_in, v_in, mask_in, w, m, v, norm_out, out, prow, r1, r2,
                lr, own, par, st1, st2, early, mask, sb, r3, acc, nrm,
                psend, precv, sent, s1r, s2r, s3r, ns, nr, lo, lp, l1, l2, ld, is_, ir, ds_, dr):
    me = lax.axis_index('dp')
    partner = me + 1 - 2 * (me % 2)
    near = [me + step_of(me, a) for a in range(3)]

    base_of = {1: 0, 2: 48, 3: 72, 4: 84}
    count_of = {1: 48, 2: 24, 3: 12, 4: 12}

    def decode(phase, t):
        if phase == 1:
            if isinstance(t, int) and t < 12:
                return t % 3, 0, t // 3
            return (t // 4) % 3, t // 12, t % 4
        if phase == 2:
            return (t // 2) % 3, t // 6, t % 2
        return t % 3, t // 3, 0

    def where(phase, t):
        p, k, j = decode(phase, t)
        if phase == 1:
            o1, o2, o3 = 1, j % 2, j // 2
        elif phase == 2:
            o1, o2, o3 = 0, 1, j
        else:
            o1, o2, o3 = 0, 0, 1 if phase == 3 else 0
        shift = o1 * step_of(me, p) + o2 * step_of(me, (p + 1) % 3) + o3 * step_of(me, (p + 2) % 3)
        return shift, 4 * p + k

    def grad_slice(block, q):
        start = pl.multiple_of((block * ROWS + chunk_row(q)) * LANES, LANES)
        return grad.at[:, pl.ds(start, CW)]

    def early_copy(t):
        shift, q = where(1, t)
        return remote(grad_slice(partner + shift, q), early.at[t], psend, precv.at[LATE + 1 + t], partner)

    def partner_copy(phase, t):
        shift, q = where(phase, t)
        group = t // 4 if phase == 1 else LATE
        return remote(grad_slice(partner + shift, q), prow.at[base_of[phase] + t], psend, precv.at[group], partner)

    def rows_here(first, count, group):
        rows = prow.at[pl.ds(first, count)]
        return remote(rows, rows, psend, precv.at[group], partner)

    def own_load(phase, t):
        shift, q = where(phase, t)
        slot = t % DEPTH
        return pltpu.make_async_copy(grad_slice(me + shift, q), own.at[slot], lo.at[slot])

    def slots(g, count):
        return sb.at[pl.ds(4 * (g % GROUPS), count)]

    def s1_one(p, j):
        return remote(sb.at[4 * p + j], r1.at[16 * p + j], sent.at[p], s1r.at[4 * p], me + step_of(me, p))

    def s1_copy(p, k):
        g = 3 * k + p
        return remote(slots(g, 4), r1.at[pl.ds((4 * p + k) * 4, 4)], sent.at[g % GROUPS], s1r.at[4 * p + k], me + step_of(me, p))

    def s2_copy(p, k):
        g = 3 * k + p
        return remote(slots(g, 2), r2.at[pl.ds((4 * p + k) * 2, 2)], sent.at[g % GROUPS], s2r.at[4 * p + k], me + step_of(me, (p + 1) % 3))

    def s3_copy(p, k):
        g = 3 * k + p
        return remote(sb.at[4 * (g % GROUPS)], r3.at[g], sent.at[g % GROUPS], s3r.at[g], me + step_of(me, (p + 2) % 3))

    def left(g, count):
        here = slots(g, count)
        remote(here, here, sent.at[g % GROUPS], s1r.at[0], partner).wait_send()

    def sources(phase, t):
        p, k, j = decode(phase, t)
        q = 4 * p + k
        if phase == 2:
            return 4 * q + 2 * j + 1, None
        if phase == 3:
            return 4 * q + 2, 2 * q + 1
        return 4 * q, 2 * q

    def loads(phase, t):
        slot = t % DEPTH
        copies = [own_load(phase, t), pltpu.make_async_copy(prow.at[base_of[phase] + t], par.at[slot], lp.at[slot])]
        if phase > 1:
            i1, i2 = sources(phase, t)
            copies.append(pltpu.make_async_copy(r1.at[i1], st1.at[slot], l1.at[slot]))
            if phase > 2:
                copies.append(pltpu.make_async_copy(r2.at[i2], st2.at[slot], l2.at[slot]))
        return copies

    def when(cond, fn):
        if isinstance(cond, bool):
            if cond:
                fn()
        else:
            pl.when(cond)(fn)

    def start_loads(phase, t):
        p, k, j = decode(phase, t)
        if phase == 1:
            when(t % 4 == 0, lambda: rows_here(t, 4, t // 4).wait_recv())
        elif phase == 2:
            when(j == 0, lambda: s1_copy(p, k).wait_recv())
        elif phase == 3:
            s2_copy(p, k).wait_recv()
        for c in loads(phase, t):
            c.start()

    def chip_sum(slot, i, rows_of=None):
        rows_of = par if rows_of is None else rows_of
        cols = pl.ds(pl.multiple_of(i * (SLAB * LANES), SLAB * LANES), SLAB * LANES)
        total = own[slot, :, cols].astype(jnp.float32) + rows_of[slot, :, cols].astype(jnp.float32)
        return total.reshape(SLAB, LANES)

    def slabs(fn):
        def one(i, _):
            fn(i, pl.ds(pl.multiple_of(i * SLAB, SLAB), SLAB))
            return 0
        lax.fori_loop(0, NSLAB, one, 0)

    def loop(lo_t, hi_t, fn):
        def one(t, _):
            fn(t)
            return 0
        lax.fori_loop(lo_t, hi_t, one, 0)

    def run_phase(phase, body, first=0, static=0):
        n = count_of[phase]
        for t in range(first, first + DEPTH - 1):
            start_loads(phase, t)

        def one(t):
            when(t + DEPTH - 1 < n, lambda: start_loads(phase, t + DEPTH - 1))
            for c in loads(phase, t):
                c.wait()
            body(t)
        for t in range(first, static):
            one(t)
        loop(max(first, static), n, one)

    barrier = pltpu.get_barrier_semaphore()
    for other in [partner] + near:
        pl.semaphore_signal(barrier, inc=1, device_id=(other,), device_id_type=MESH)
    for t in range(DEPTH):
        own_load(1, t).start()
    pl.semaphore_wait(barrier, 4)

    for t in range(DEPTH):
        early_copy(t).start()
    for t in range(DEPTH):
        own_load(1, t).wait()
        early_copy(t).wait_recv()
        p, k, j = decode(1, t)

        def fn(i, rows):
            sb[4 * p + j, rows, :] = chip_sum(t, i, early)
        slabs(fn)
        s1_one(p, j).start()
        if t == 0:
            for u in range(DEPTH, 12):
                partner_copy(1, u).start()
    loop(12, 48, lambda t: partner_copy(1, t).start())

    def phase1(t):
        p, k, j = decode(1, t)
        g = 3 * k + p
        if not isinstance(t, int):
            when((t >= 24) & (j == 0), lambda: left(g, 4))
        slot = t % DEPTH

        def fn(i, rows):
            sb[4 * (g % GROUPS) + j, rows, :] = chip_sum(slot, i)
        slabs(fn)
        if isinstance(t, int):
            s1_one(p, j).start()
        else:
            when(j == 3, lambda: s1_copy(p, k).start())

    def phase2(t):
        p, k, j = decode(2, t)
        g = 3 * k + p
        when((j == 0) & (t < 12), lambda: left(g, 4))
        when((j == 0) & (t >= 12), lambda: left(g, 2))
        slot = t % DEPTH

        def fn(i, rows):
            sb[4 * (g % GROUPS) + j, rows, :] = chip_sum(slot, i) + st1[slot, rows, :]
        slabs(fn)
        when(j == 1, lambda: s2_copy(p, k).start())

    def phase3(t):
        p, k, _ = decode(3, t)
        when(t < 6, lambda: left(t, 2))
        when(t >= 6, lambda: left(t, 1))
        slot = t % DEPTH

        def fn(i, rows):
            sb[4 * (t % GROUPS), rows, :] = chip_sum(slot, i) + st1[slot, rows, :] + st2[slot, rows, :]
        slabs(fn)
        s3_copy(p, k).start()

    def early_sum(t):
        return 4 * (t // 3) + 1 + t % 3

    def phase4(t):
        slot = t % DEPTH

        def fn(i, rows):
            sb[early_sum(t), rows, :] = chip_sum(slot, i) + st1[slot, rows, :] + st2[slot, rows, :]
        slabs(fn)

    run_phase(1, phase1, DEPTH, 12)
    for phase in (2, 3, 4):
        loop(0, count_of[phase], lambda t, phase=phase: partner_copy(phase, t).start())
    rows_here(48, 48, LATE).wait_recv()

    pairs = ((w_in, w), (m_in, m), (v_in, v), (mask_in, mask), (lr_in, lr))
    states = [pltpu.make_async_copy(a, b, ld.at[i]) for i, (a, b) in enumerate(pairs)]
    for c in states:
        c.start()
    run_phase(2, phase2)
    for c in states:
        c.wait()
    rows_here(DEPTH, 96 - DEPTH, LATE).wait_send()
    remote(early, early, psend, precv.at[0], partner).wait_send()
    run_phase(3, phase3)
    run_phase(4, phase4)

    acc[...] = jnp.zeros_like(acc)

    def finish(t, skip):
        s3_copy(t % 3, t // 3).wait_recv()

        def fn(i, rows):
            g = (sb[early_sum(t), rows, :] + r3[t, rows, :]) * (1.0 / NDEV)
            r3[t, rows, :] = g
            sq = g * g
            if skip:
                row = lax.broadcasted_iota(jnp.int32, (SLAB, LANES), 0) + i * SLAB
                sq = jnp.where(row < skip, 0.0, sq)
            acc[...] += jnp.sum(sq.reshape(SLAB // 8, 8, LANES), axis=0)
        slabs(fn)

    loop(0, 11, lambda t: finish(t, 0))
    finish(11, 4)

    nrm[me] = acc[...]

    def norm_copy(i):
        return remote(acc, nrm.at[me], ns, nr, lax.rem(me + i, NDEV))

    others = nrm.at[pl.ds(0, NDEV - 1)]
    all_norms = remote(others, others, ns, nr, partner)
    loop(1, NDEV, lambda i: norm_copy(i).start())
    for g in range(6, 12):
        left(g, 1)
    all_norms.wait_recv()
    total = nrm[0]
    for i in range(1, NDEV):
        total = total + nrm[i]
    norm = jnp.sqrt(jnp.sum(total, keepdims=True))
    norm_out[...] = jnp.broadcast_to(norm, norm_out.shape)
    clip = jnp.minimum(1.0, 1.0 / (norm + CLIP_EPS))
    rate = lr[...].reshape(1, 1)

    def block_of(p, n):
        block = me
        for bit in range(3):
            if (n >> bit) & 1:
                block = block + step_of(me, (p + bit) % 3)
        return block

    def end_of(p, k):
        return min(AG_UNITS * (4 * p + k), UNITS)

    def place(p, n, k0, k1):
        return out.at[pl.ds(block_of(p, n) * UNITS + end_of(p, k0), end_of(p, k1) - end_of(p, k0))]

    def ir_index(p, n, k0):
        return 21 + p if (n == 7 and k0) else 3 * (n - 1) + p

    def ici(p, n, hop, k0, k1):
        here = place(p, n, k0, k1)
        return remote(here, here, is_, ir.at[ir_index(p, n | (1 << hop), k0)], near[(p + hop) % 3])

    def arrival(p, n, k0=0, k1=4):
        here = place(p, n, k0, k1)
        return remote(here, here, is_, ir.at[ir_index(p, n, k0)], partner)

    def die(here):
        return remote(here, here, ds_, dr, partner)

    def update(p, k):
        t = 3 * k + p
        q = 4 * p + k
        short = q == CHUNKS - 1

        def slab(row0, n):
            rows = pl.ds(row0 + q * CR, n)
            src = pl.ds(row0 + 4, n) if short else pl.ds(row0, n)
            w_new, m_new, v_new = adam_slab(rate, clip, r3[t, src, :], w[rows, :], m[rows, :], v[rows, :], mask[rows, :])
            w[rows, :] = w_new
            m[rows, :] = m_new
            v[rows, :] = v_new
            return w_new.astype(jnp.bfloat16).reshape(n // 4, 4, LANES)

        base = me * UNITS + q * AG_UNITS
        if short:
            for i in range(0, CR, SLAB):
                n = min(SLAB, ROWS - q * CR - i)
                out[pl.ds(base + i // 4, n // 4)] = slab(i, n)
        else:
            def one(i, _):
                out[pl.ds(base + i * (SLAB // 4), SLAB // 4)] = slab(pl.multiple_of(i * SLAB, SLAB), SLAB)
                return 0
            lax.fori_loop(0, NSLAB, one, 0)

    for p in range(3):
        update(p, 0)
        for hop in range(3):
            ici(p, 0, hop, 0, 1).start()
    for k in range(1, 4):
        for p in range(3):
            update(p, k)
            ici(p, 0, 0, k, k + 1).start()
    for hop in (1, 2):
        for p in range(3):
            ici(p, 0, hop, 1, 4).start()
    die(out.at[pl.ds(me * UNITS, UNITS)]).start()
    all_norms.wait_send()

    def pass_on(n, hops):
        for p in range(3):
            arrival(p, n).wait_recv()
            for hop in hops:
                if n | (1 << hop) == 7:
                    ici(p, n, hop, 0, 3).start()
                    ici(p, n, hop, 3, 4).start()
                else:
                    ici(p, n, hop, 0, 4).start()
            die(place(p, n, 0, 4)).start()

    pass_on(1, (1, 2))
    pass_on(2, (2,))
    pass_on(3, (2,))
    pass_on(4, ())
    pass_on(5, ())
    pass_on(6, ())
    for k0, k1 in ((0, 3), (3, 4)):
        for p in range(3):
            arrival(p, 7, k0, k1).wait_recv()
            die(place(p, 7, k0, k1)).start()
    sends = out.at[pl.ds(0, 7 * UNITS)]
    remote(sends, sends, is_, ir.at[0], partner).wait_send()
    half = out.at[pl.ds(0, 8 * UNITS)]
    die(half).wait_send()
    die(half).wait_recv()


def step(lr, grad, w, m, v, mask):
    f32, bf16 = jnp.float32, jnp.bfloat16
    dma = pltpu.SemaphoreType.DMA
    flat = lambda a: pltpu.with_memory_space_constraint(a.reshape(ROWS, LANES), pltpu.HBM)
    hbm = pl.BlockSpec(memory_space=pl.ANY)
    vmem = pl.BlockSpec(memory_space=pltpu.VMEM)
    state = pltpu.VMEM((ROWS, LANES), f32)
    return pl.pallas_call(
        step_kernel,
        out_shape=(
            state, state, state, pltpu.VMEM((8, LANES), f32),
            pltpu.VMEM((NDEV * UNITS, 4, LANES), bf16),
            pltpu.HBM((96, 1, CW), bf16), pltpu.HBM((48, CR, LANES), f32), pltpu.HBM((24, CR, LANES), f32),
        ),
        in_specs=[hbm] * 6,
        out_specs=(vmem, vmem, vmem, vmem, vmem, hbm, hbm, hbm),
        scratch_shapes=[
            pltpu.VMEM((1,), f32),
            pltpu.VMEM((DEPTH, 1, CW), bf16),
            pltpu.VMEM((DEPTH, 1, CW), bf16),
            pltpu.VMEM((DEPTH, CR, LANES), f32),
            pltpu.VMEM((DEPTH, CR, LANES), f32),
            pltpu.VMEM((DEPTH, 1, CW), bf16),
            pltpu.VMEM((ROWS, LANES), jnp.int32),
            pltpu.VMEM((4 * GROUPS, CR, LANES), f32),
            pltpu.VMEM((12, CR, LANES), f32),
            pltpu.VMEM((8, LANES), f32),
            pltpu.VMEM((NDEV, 8, LANES), f32),
            dma(()), dma((LATE + 1 + DEPTH,)), dma((GROUPS,)),
            dma((12,)), dma((12,)), dma((12,)),
            dma(()), dma(()),
            dma((DEPTH,)), dma((DEPTH,)), dma((DEPTH,)), dma((DEPTH,)),
            dma((5,)),
            dma(()), dma((24,)), dma(()), dma(()),
        ],
        compiler_params=pltpu.CompilerParams(collective_id=0, has_side_effects=True, vmem_limit_bytes=22 * 1024 * 1024),
        name='step',
    )(lr, grad, flat(w), flat(m), flat(v), flat(mask))


PUBLISH_PIECES = 8


def publish_kernel(p_in, w_in, m_in, v_in, n_in, p_out, w_out, m_out, v_out, n_out, big, small):
    size = NDEV * UNITS // PUBLISH_PIECES
    copies = [pltpu.make_async_copy(p_in.at[pl.ds(i * size, size)], p_out.at[pl.ds(i * size, size)], big.at[i]) for i in range(PUBLISH_PIECES)]
    copies += [pltpu.make_async_copy(a, b, small.at[i]) for i, (a, b) in enumerate(((w_in, w_out), (m_in, m_out), (v_in, v_out)))]
    for c in copies:
        c.start()
    n_out[...] = n_in[0, 0:1]
    for c in copies:
        c.wait()


def publish(arrays, norm):
    dma = pltpu.SemaphoreType.DMA
    vmem = pl.BlockSpec(memory_space=pltpu.VMEM)
    hbm = pl.BlockSpec(memory_space=pl.ANY)
    arrays = [pltpu.with_memory_space_constraint(a, pltpu.VMEM) for a in arrays]
    norm = pltpu.with_memory_space_constraint(norm, pltpu.VMEM)
    return pl.pallas_call(
        publish_kernel,
        out_shape=[jax.ShapeDtypeStruct(a.shape, a.dtype) for a in arrays] + [jax.ShapeDtypeStruct((1,), jnp.float32)],
        in_specs=[vmem] * 5,
        out_specs=[hbm] * 4 + [vmem],
        scratch_shapes=[dma((PUBLISH_PIECES,)), dma((3,))],
        compiler_params=pltpu.CompilerParams(vmem_limit_bytes=1024 * 1024),
        name='publish',
    )(*arrays, norm)


def solution(mesh):
    def local_step(grad_row, master, mom_first, mom_second, decay_mask, learn_rate):
        w, m, v, norm, params, *_ = step(learn_rate, grad_row, master, mom_first, mom_second, decay_mask)
        params, w, m, v, norm = publish([params, w, m, v], norm)
        return params.reshape(-1), w.reshape(-1), m.reshape(-1), v.reshape(-1), norm

    return jax.shard_map(local_step, mesh=mesh, in_specs=(P('dp', None), P('dp'), P('dp'), P('dp'), P('dp'), P()), out_specs=(P(), P('dp'), P('dp'), P('dp'), P()), check_vma=False)
```

time: 298 us -> 298 us (level)
  no operation moved by 1% of the time
where the time goes in v4:
time: 298 us; the launch traced here: 297 us
  Pallas kernels  296 us (99%)
    pallas_call x1, Pallas kernels, step(): pl.pallas_call(step_kernel, out_shape=(state, state, state, pltpu.VMEM((8...  283 us
    pallas_call x1, Pallas kernels, publish(): pl.pallas_call(publish_kernel, out_shape=[jax.ShapeDtypeStruct(a.shape, a...  13.2 us

profile of v4, /device:TPU:0, one launch (start us, length us, event | category | flops | bytes accessed | tf_op | source)
XLA Modules:
  0.0 297.5 jit_solution(7532795534988000225)
XLA Ops:
  1.3 283.0 %step.1 = (f32[6908,128]{1,0:T(8,128)S(1)}, f32[6908,128]{1,0:T(8,128)S(1)}, f32[6908,128]{1,0:T(8,128)S(1)}, f32[8,128]{1,0:T(8,128)S(1)}, bf16[27632,4,128]{2,...) custom-call(f32[1]{0:T(128)S(6)} %copy.11.lr_in, ...), custom_call_target="tpu_custom_call" | custom-call | tf_op jit(solution)/shard_map/step/pallas_call | solution.py:428
  284.3 13.2 %publish.1 = (bf16[27632,4,128]{2,1,0:T(4,128)(2,1)}, f32[6908,128]{1,0:T(8,128)}, f32[6908,128]{1,0:T(8,128)}, f32[6908,128]{1,0:T(8,128)}, f32[1]{0:T(128)}) custom-call(bf16[27632,4,128]{2,1,0:T(4,128)(2,1)S(1)} %get-tuple-element.15.p_in, f32[6908,128]{1,0:T(8,128)S(1)} %get-tuple-element.16.w_in, f32[6908,128]{1,0:T(8,128)S(1)} %get-tuple-element.17.m_in, ...), custom_call_target="tpu_custom_call" | custom-call | tf_op jit(solution)/shard_map/publish/pallas_call | solution.py:481
